TPU v7x, 256 devices: a whole 4x4x8 slice. The times are simulated.
256 devices in a mesh: table: 4 (over z_lo), row: 64 (over z_hi, y, x, core).
Axes of the slice: x: 4, y: 4, z: 8 (z_hi: 2, z_lo: 4; z = z_hi * 4 + z_lo), core: 2. Of those that a mesh axis runs over, the one named last changes fastest.
Arguments:
- tables: bfloat16 [4, 524288, 128], P('table', 'row'), may hold values from -3 to 3
- indices: int32 [4, 100, 512], P('table'), may hold values from 0 to 524287
- weights: bfloat16 [4, 100, 512], P('table'), may hold values from 0.19921875 to 1
- lengths: int32 [4, 512], P('table'), may hold values from 1 to 100, as said below
Outputs:
- pooled: bfloat16 [4, 512, 128], P(None, ('table', 'row'))
Inputs may be any that keep to these rules, and one draw needn't show every extreme that they name: `lengths`: the longest bag of each table has a power of two of at most 64 positions, or 100 positions, and some table has a bag of 100.
All inputs are finite; a program needn't handle non-finite values.
Results may differ from a plain program's by a relative error of at most 0.001.
Values may be sent and summed in bfloat16 or wider, within the bound.
A program may use at most 64 MiB of HBM per device.

v0:
```python
import functools

import jax
import jax.numpy as jnp
from jax import lax
from jax.experimental import pallas as pl
from jax.experimental.pallas import tpu as pltpu
from jax.sharding import PartitionSpec as P

MESH = pl.DeviceIdType.MESH
LANES = 128
BLOCK = 8
PAIR = 2
VOTERS = 3
F32 = jnp.float32
BF16 = jnp.bfloat16
I32 = jnp.int32


def pool_kernel(
    t_hbm, i_hbm, w_hbm, l_hbm, out_ref,
    t_bf, t_f32, idx_ref, wt_ref, len_ref, pos_ref, val_ref, slot_ref, rows_ref, gathered, slot_smem,
    t_sem, in_sem, smem_sem,
):
    rows, width = t_f32.shape
    bag, batch = wt_ref.shape
    padded = pos_ref.shape[0]
    tiles = batch // LANES
    chunks = t_sem.shape[0]
    chunk = rows // chunks

    def table_copy(c):
        part = pl.ds(c * chunk, chunk)
        return pltpu.make_async_copy(t_hbm.at[0, part], t_bf.at[part], t_sem.at[c])

    copies = [
        pltpu.make_async_copy(i_hbm, idx_ref, in_sem.at[0]),
        pltpu.make_async_copy(w_hbm.at[0], wt_ref, in_sem.at[1]),
        pltpu.make_async_copy(l_hbm, len_ref, in_sem.at[2]),
    ]
    for copy in copies:
        copy.start()
    for c in range(chunks):
        table_copy(c).start()
    pos_ref[bag:padded, :] = jnp.full((padded - bag, batch), -1, I32)
    val_ref[bag:padded, :] = jnp.zeros((padded - bag, batch), I32)
    for copy in copies:
        copy.wait()

    first_row = lax.axis_index("row") * rows
    position = lax.broadcasted_iota(I32, (bag, LANES), 0)
    lane_tiles = [slice(tile * LANES, (tile + 1) * LANES) for tile in range(tiles)]
    locals_, insides = [], []
    for tile, lanes in enumerate(lane_tiles):
        local = idx_ref[pl.ds(tile, bag, stride=tiles), :] - first_row
        inside = (local >= 0) & (local < rows) & (position < len_ref[0:1, lanes])
        locals_.append(local)
        insides.append(inside)

    bits = (rows - 1).bit_length()
    votes = [jnp.zeros((8, LANES), I32) for _ in range(bits + 1)]
    for local, inside in zip(locals_, insides):
        for r in range(VOTERS):
            part = slice(r * 8, r * 8 + 8)
            ballot = jnp.where(inside[part], local[part] + rows, 0)
            for b in range(bits + 1):
                votes[b] = votes[b] + ((ballot >> b) & 1)
    tally = jnp.dot(
        jnp.concatenate(votes, axis=0).astype(F32).astype(BF16),
        jnp.ones((LANES, LANES), BF16),
        preferred_element_type=F32,
    ).reshape(bits + 1, 8, LANES).sum(axis=1)
    leader = jnp.zeros((1, LANES), I32)
    for b in range(bits):
        leader = leader + jnp.where(2.0 * tally[b : b + 1] > tally[bits : bits + 1], 1 << b, 0)

    lower = lax.broadcasted_iota(I32, (bag, bag), 0) >= lax.broadcasted_iota(I32, (bag, bag), 1)
    lower = jnp.where(lower, 1.0, 0.0).astype(BF16)
    base = jnp.zeros((1, LANES), F32)
    lead_weights = []
    for tile, lanes in enumerate(lane_tiles):
        local, inside = locals_[tile], insides[tile]
        weight = wt_ref[:, lanes].astype(F32)
        leads = inside & (local == leader)
        lead_weights.append(jnp.where(leads, weight, 0.0).sum(axis=0, keepdims=True))
        inside = inside & (local != leader)
        ones = jnp.where(inside, 1.0, 0.0).astype(BF16)
        count = jnp.dot(lower, ones, preferred_element_type=F32)
        pos_ref[:bag, lanes] = jnp.where(inside, count + (base - 1.0), -1.0).astype(I32)
        milli = (weight * 1024.0).astype(I32)
        val_ref[:bag, lanes] = local + milli * 32768 + tile * 8192
        base = base + count[bag - 1 : bag, :]
    slot_rows = jnp.max(base).astype(I32)
    lead_row = jnp.max(leader)
    lead_columns = jnp.concatenate(lead_weights + [jnp.zeros((8 - tiles, LANES), F32)], axis=0).T

    def smem_copy(slot):
        return pltpu.make_async_copy(rows_ref.at[slot], slot_smem.at[slot], smem_sem.at[slot])

    def select(block, slot):
        first = block * BLOCK
        totals = [jnp.zeros((8, LANES), I32) for _ in range(BLOCK)]
        for lanes in lane_tiles:
            for r in range(padded // 8):
                here = pos_ref[r * 8 : r * 8 + 8, lanes] - first
                value = val_ref[r * 8 : r * 8 + 8, lanes]
                for k in range(BLOCK):
                    totals[k] = totals[k] + jnp.where(here == k, value, 0)
        packed = jnp.concatenate([t.sum(axis=0, keepdims=True) for t in totals], axis=0)
        slot_ref[slot] = packed
        rows_ref[slot] = packed & 8191
        smem_copy(slot).start()

    blocks = (slot_rows + (BLOCK - 1)) // BLOCK

    @pl.when(blocks > 0)
    def _():
        select(0, 0)

    for c in range(chunks):
        table_copy(c).wait()
        t_f32[c * chunk : (c + 1) * chunk, :] = t_bf[c * chunk : (c + 1) * chunk, :].astype(F32)
    lead_values = t_f32[pl.ds(lead_row, 1), :]
    for tile, lanes in enumerate(lane_tiles):
        out_ref[lanes, :] = lead_columns[:, tile : tile + 1] * lead_values

    diagonal = lax.broadcasted_iota(I32, (LANES, LANES), 0) == lax.broadcasted_iota(
        I32, (LANES, LANES), 1
    )

    @pl.loop(0, blocks)
    def _(block):
        slot = lax.rem(block, 2)

        @pl.when(block + 1 < blocks)
        def _():
            select(block + 1, 1 - slot)

        smem_copy(slot).wait()
        pairs = (jnp.minimum(slot_rows - block * BLOCK, BLOCK) + (PAIR - 1)) // PAIR

        @pl.loop(0, pairs)
        def _(pair):
            packed = []
            for k in range(PAIR):
                row = pair * PAIR + k
                for u in range(LANES):
                    source = slot_smem[slot, row, u]
                    gathered[k * LANES + u : k * LANES + u + 1, :] = t_f32[pl.ds(source, 1), :]
                packed.append(slot_ref[slot, pl.ds(row, 1), :])
            values = gathered[...].astype(BF16)
            for tile, lanes in enumerate(lane_tiles):
                parts = []
                for p in packed:
                    weight = (p >> 15).astype(F32) * (1.0 / 1024.0)
                    weight = jnp.where(((p >> 13) & 3) == tile, weight, 0.0)
                    parts.append(jnp.where(diagonal, weight, 0.0).astype(BF16))
                out_ref[lanes, :] += jnp.dot(
                    jnp.concatenate(parts, axis=1), values, preferred_element_type=F32
                )


def pool(tables, indices, weights, lengths):
    rows, width = tables.shape[1:]
    bag, batch = indices.shape[1:]
    padded = (bag + 7) // 8 * 8
    tiles = batch // LANES
    return pl.pallas_call(
        pool_kernel,
        out_shape=jax.ShapeDtypeStruct((batch, width), F32),
        in_specs=[pl.BlockSpec(memory_space=pltpu.HBM)] * 4,
        out_specs=pl.BlockSpec(memory_space=pltpu.VMEM),
        scratch_shapes=[
            pltpu.VMEM((rows, width), BF16),
            pltpu.VMEM((rows, width), F32),
            pltpu.VMEM((bag * tiles, LANES), I32),
            pltpu.VMEM((bag, batch), BF16),
            pltpu.VMEM((1, batch), I32),
            pltpu.VMEM((padded, batch), I32),
            pltpu.VMEM((padded, batch), I32),
            pltpu.VMEM((2, BLOCK, LANES), I32),
            pltpu.VMEM((2, BLOCK, LANES), I32),
            pltpu.VMEM((PAIR * LANES, width), F32),
            pltpu.SMEM((2, BLOCK, LANES), I32),
            pltpu.SemaphoreType.DMA((4,)),
            pltpu.SemaphoreType.DMA((3,)),
            pltpu.SemaphoreType.DMA((2,)),
        ],
        compiler_params=pltpu.CompilerParams(vmem_limit_bytes=24 * 1024 * 1024),
        name="pool",
    )(tables, pltpu.with_memory_space_constraint(indices.reshape(bag * tiles, LANES), pltpu.HBM), weights, lengths)


def exchange_kernel(tables, p_ref, out_ref, recv1, send2, recv2, s1_send, s1_recv, s2_send, s2_recv):
    groups = recv1.shape[0]
    ends = recv2.shape[0]
    high = ends // tables
    table, row = lax.axis_index("table"), lax.axis_index("row")
    plane, place = row // groups, lax.rem(row, groups)

    def plane_peer(d):
        return lax.rem(place + d, groups)

    def line_peer(d):
        return lax.rem(table + d // high, tables), lax.rem(plane + d % high, high)

    barrier = pltpu.get_barrier_semaphore()
    for d in range(1, groups):
        pl.semaphore_signal(
            barrier, inc=1, device_id=(table, plane * groups + plane_peer(d)), device_id_type=MESH
        )
    for d in range(1, ends):
        t, h = line_peer(d)
        pl.semaphore_signal(barrier, inc=1, device_id=(t, h * groups + place), device_id_type=MESH)
    pl.semaphore_wait(barrier, groups + ends - 2)

    def first_copy(d):
        peer = plane_peer(d)
        return pltpu.make_async_remote_copy(
            src_ref=p_ref.at[:, peer],
            dst_ref=recv1.at[d],
            send_sem=s1_send.at[d],
            recv_sem=s1_recv.at[d],
            device_id=(table, plane * groups + peer),
            device_id_type=MESH,
        )

    for d in range(1, groups):
        first_copy(d).start()
    total = p_ref[:, place]
    for d in range(1, groups):
        first_copy(d).wait_recv()
        total = total + recv1[d]
    send2[...] = total

    def second_copy(d):
        t, h = line_peer(d)
        return pltpu.make_async_remote_copy(
            src_ref=send2.at[t * high + h],
            dst_ref=recv2.at[d],
            send_sem=s2_send.at[d],
            recv_sem=s2_recv.at[d],
            device_id=(t, h * groups + place),
            device_id_type=MESH,
        )

    for d in range(1, ends):
        second_copy(d).start()
    recv2[0] = send2[table * high + plane]
    for d in range(1, ends):
        second_copy(d).wait_recv()
    for dt in range(tables):
        source = lax.rem(table - dt + tables, tables)
        value = recv2[dt * high]
        for dh in range(1, high):
            value = value + recv2[dt * high + dh]
        out_ref[source] = value.astype(BF16)
    for d in range(1, groups):
        first_copy(d).wait_send()
    for d in range(1, ends):
        second_copy(d).wait_send()


def exchange(partial, tables, groups, ends):
    batch, width = partial.shape
    each = batch // (groups * ends)
    return pl.pallas_call(
        functools.partial(exchange_kernel, tables),
        out_shape=jax.ShapeDtypeStruct((tables, each, width), BF16),
        in_specs=[pl.BlockSpec(memory_space=pltpu.VMEM)],
        out_specs=pl.BlockSpec(memory_space=pltpu.VMEM),
        scratch_shapes=[
            pltpu.VMEM((groups, ends, each, width), F32),
            pltpu.VMEM((ends, each, width), F32),
            pltpu.VMEM((ends, each, width), F32),
            pltpu.SemaphoreType.DMA((groups,)),
            pltpu.SemaphoreType.DMA((groups,)),
            pltpu.SemaphoreType.DMA((ends,)),
            pltpu.SemaphoreType.DMA((ends,)),
        ],
        compiler_params=pltpu.CompilerParams(
            collective_id=0, has_side_effects=True, vmem_limit_bytes=24 * 1024 * 1024
        ),
        name="exchange",
    )(partial.reshape(ends, groups, each, width))


def on_device(tables, indices, weights, lengths):
    tables, weights, lengths = [pltpu.with_memory_space_constraint(x, pltpu.HBM) for x in (tables, weights, lengths)]
    partial = pool(tables, indices, weights, lengths)
    return exchange(partial, lax.axis_size("table"), 32, 8)


def solution(mesh):
    placed = (
        P("table", "row", None),
        P("table", None, None),
        P("table", None, None),
        P("table", None),
    )
    return jax.shard_map(
        on_device,
        mesh=mesh,
        in_specs=placed,
        out_specs=P(None, ("table", "row"), None),
        check_vma=False,
    )
```

profile of v0, /device:TPU:1, one launch (start us, length us, event | category | flops | bytes accessed | tf_op | source)
XLA Modules:
  0.0 25.9 jit_solution(10140831568407474635)
XLA Ops:
  0.0 3.2 %pool.1 = f32[512,128]{1,0:T(8,128)S(1)} custom-call(bf16[1,8192,128]{2,1,0:T(8,128)(2,1)} %t_hbm.1, s32[400,128]{1,0:T(8,128)} %bitcast.3, bf16[1,100,512]{2,1,0:T(8,128)(2,1)} %w_hbm.1, s32[1,512]{1,0:T(1,128)} %l_hbm.1), custom_call_target="tpu_custom_call" | custom-call | tf_op jit(solution)/shard_map/pool/pallas_call | solution.py:168
  3.2 22.1 %exchange.1 = bf16[4,2,128]{2,1,0:T(2,128)(2,1)S(1)} custom-call(f32[8,32,2,128]{3,2,1,0:T(2,128)S(1)} %bitcast.2), custom_call_target="tpu_custom_call" | custom-call | tf_op jit(solution)/shard_map/exchange/pallas_call | solution.py:267
  25.3 0.6 %copy.6 = bf16[4,2,128]{2,1,0:T(2,128)(2,1)} copy(bf16[4,2,128]{2,1,0:T(2,128)(2,1)S(1)} %exchange.1) | data formatting | bytes 4096
where the time goes:
time: 25.9 us
  Pallas kernels  25.3 us (98%)
  local copies, waits for them, and re-layouts  0.58 us (2%)
    pallas_call x1, Pallas kernels, exchange(): pl.pallas_call(functools.partial(exchange_kernel, tables), out_shape=jax....  22.1 us
    pallas_call x1, Pallas kernels, pool(): pl.pallas_call(pool_kernel, out_shape=jax.ShapeDtypeStruct((batch, width)...  3.22 us
    unnamed x1, local copies, waits for them, and re-layouts  0.58 us

commit v1 on v0

v1 whole, which is shorter than its diff:
```python
import functools

import jax
import jax.numpy as jnp
from jax import lax
from jax.experimental import pallas as pl
from jax.experimental.pallas import tpu as pltpu
from jax.sharding import PartitionSpec as P

MESH = pl.DeviceIdType.MESH
LANES = 128
BLOCK = 8
KEEP = 16
PAIR = 2
UNROLL = 256
VOTERS = 3
F32 = jnp.float32
BF16 = jnp.bfloat16
I32 = jnp.int32


def bag_places(batch):
    lane = lax.broadcasted_iota(I32, (1, LANES), 1)
    return ((lane >> 1) & 31) * 16 + (lane >> 6) * 2 + (lane & 1)


def pick_bags(packed, batch):
    lane_place = bag_places(batch)
    place = jnp.concatenate([lane_place + ((p >> 13) & 3) * 4 for p in packed], axis=1)
    weight = jnp.concatenate([(p >> 15).astype(F32) * (1.0 / 1024.0) for p in packed], axis=1)
    rows = lax.broadcasted_iota(I32, (batch, place.shape[1]), 0)
    return jnp.where(rows == place, weight, 0.0).astype(BF16)


def rank_kernel(
    t_hbm, i_hbm, w_hbm, l_hbm, keep_ref, ids_ref, lead_ref, over_ref,
    t_bf, t_f32, idx_ref, wt_ref, len_ref, pos_ref, val_ref, slot_ref, rows_ref, gathered, slot_smem,
    t_sem, in_sem, smem_sem,
):
    rows, width = t_f32.shape
    bag, batch = wt_ref.shape
    padded = pos_ref.shape[0]
    tiles = batch // LANES

    copies = [
        pltpu.make_async_copy(i_hbm, idx_ref, in_sem.at[0]),
        pltpu.make_async_copy(w_hbm.at[0], wt_ref, in_sem.at[1]),
        pltpu.make_async_copy(l_hbm, len_ref, in_sem.at[2]),
    ]
    for copy in copies:
        copy.start()
    pos_ref[bag:padded, :] = jnp.full((padded - bag, batch), -1, I32)
    val_ref[bag:padded, :] = jnp.zeros((padded - bag, batch), I32)
    over_ref[...] = jnp.zeros_like(over_ref)
    for copy in copies:
        copy.wait()

    first_row = lax.axis_index("row") * rows
    position = lax.broadcasted_iota(I32, (bag, LANES), 0)
    lane_tiles = [slice(tile * LANES, (tile + 1) * LANES) for tile in range(tiles)]
    locals_, insides = [], []
    for tile, lanes in enumerate(lane_tiles):
        local = idx_ref[pl.ds(tile, bag, stride=tiles), :] - first_row
        inside = (local >= 0) & (local < rows) & (position < len_ref[0:1, lanes])
        locals_.append(local)
        insides.append(inside)

    bits = (rows - 1).bit_length()
    votes = [jnp.zeros((8, LANES), I32) for _ in range(bits + 1)]
    for local, inside in zip(locals_, insides):
        for r in range(VOTERS):
            part = slice(r * 8, r * 8 + 8)
            ballot = jnp.where(inside[part], local[part] + rows, 0)
            for b in range(bits + 1):
                votes[b] = votes[b] + ((ballot >> b) & 1)
    tally = jnp.dot(
        jnp.concatenate(votes, axis=0).astype(F32).astype(BF16),
        jnp.ones((LANES, LANES), BF16),
        preferred_element_type=F32,
    ).reshape(bits + 1, 8, LANES).sum(axis=1)
    leader = jnp.zeros((1, LANES), I32)
    for b in range(bits):
        leader = leader + jnp.where(2.0 * tally[b : b + 1] > tally[bits : bits + 1], 1 << b, 0)

    lower = lax.broadcasted_iota(I32, (bag, bag), 0) >= lax.broadcasted_iota(I32, (bag, bag), 1)
    lower = jnp.where(lower, 1.0, 0.0).astype(BF16)
    base = jnp.zeros((1, LANES), F32)
    for tile, lanes in enumerate(lane_tiles):
        local, inside = locals_[tile], insides[tile]
        weight = wt_ref[:, lanes].astype(F32)
        leads = inside & (local == leader)
        lead_ref[tile : tile + 1, :] = jnp.where(leads, weight, 0.0).sum(axis=0, keepdims=True)
        inside = inside & (local != leader)
        ones = jnp.where(inside, 1.0, 0.0).astype(BF16)
        count = jnp.dot(lower, ones, preferred_element_type=F32)
        pos_ref[:bag, lanes] = jnp.where(inside, count + (base - 1.0), -1.0).astype(I32)
        milli = (weight * 1024.0).astype(I32)
        val_ref[:bag, lanes] = local + milli * 32768 + tile * 8192
        base = base + count[bag - 1 : bag, :]
    lead_ref[tiles:, :] = jnp.zeros((8 - tiles, LANES), F32)
    ids_ref[KEEP : KEEP + 8, :] = jnp.broadcast_to(leader, (8, LANES))

    def chosen(first):
        totals = [jnp.zeros((8, LANES), I32) for _ in range(BLOCK)]
        for lanes in lane_tiles:
            for r in range(padded // 8):
                here = pos_ref[r * 8 : r * 8 + 8, lanes] - first
                value = val_ref[r * 8 : r * 8 + 8, lanes]
                for k in range(BLOCK):
                    totals[k] = totals[k] + jnp.where(here == k, value, 0)
        return jnp.concatenate([t.sum(axis=0, keepdims=True) for t in totals], axis=0)

    for first in range(0, KEEP, BLOCK):
        packed = chosen(first)
        keep_ref[first : first + BLOCK, :] = packed
        ids_ref[first : first + BLOCK, :] = packed & 8191

    slot_rows = jnp.max(base).astype(I32) - KEEP

    @pl.when(slot_rows > 0)
    def _():
        table_copy = pltpu.make_async_copy(t_hbm.at[0], t_bf, t_sem)
        table_copy.start()

        def smem_copy(slot):
            return pltpu.make_async_copy(rows_ref.at[slot], slot_smem.at[slot], smem_sem.at[slot])

        def select(block, slot):
            packed = chosen(KEEP + block * BLOCK)
            slot_ref[slot] = packed
            rows_ref[slot] = packed & 8191
            smem_copy(slot).start()

        blocks = (slot_rows + (BLOCK - 1)) // BLOCK
        select(0, 0)
        table_copy.wait()

        @pl.loop(0, rows, step=512)
        def _(row):
            t_f32[pl.ds(row, 512), :] = t_bf[pl.ds(row, 512), :].astype(F32)

        @pl.loop(0, blocks)
        def _(block):
            slot = lax.rem(block, 2)

            @pl.when(block + 1 < blocks)
            def _():
                select(block + 1, 1 - slot)

            smem_copy(slot).wait()
            pairs = (jnp.minimum(slot_rows - block * BLOCK, BLOCK) + (PAIR - 1)) // PAIR

            @pl.loop(0, pairs)
            def _(pair):
                packed = []
                for k in range(PAIR):
                    row = pair * PAIR + k
                    for u in range(LANES):
                        source = slot_smem[slot, row, u]
                        gathered[k * LANES + u : k * LANES + u + 1, :] = t_f32[pl.ds(source, 1), :]
                    packed.append(slot_ref[slot, pl.ds(row, 1), :])
                over_ref[...] += jnp.dot(
                    pick_bags(packed, batch),
                    gathered[...].astype(BF16),
                    preferred_element_type=F32,
                )


def rank(tables, indices, weights, lengths):
    rows, width = tables.shape[1:]
    bag, batch = indices.shape[1:]
    padded = (bag + 7) // 8 * 8
    tiles = batch // LANES
    operands = (tables, indices.reshape(bag * tiles, LANES), weights, lengths)
    return pl.pallas_call(
        rank_kernel,
        out_shape=(
            jax.ShapeDtypeStruct((KEEP, LANES), I32),
            jax.ShapeDtypeStruct((KEEP + 8, LANES), I32),
            jax.ShapeDtypeStruct((8, LANES), F32),
            jax.ShapeDtypeStruct((batch, width), F32),
        ),
        in_specs=[pl.BlockSpec(memory_space=pltpu.HBM)] * 4,
        out_specs=(pl.BlockSpec(memory_space=pltpu.VMEM),) * 4,
        scratch_shapes=[
            pltpu.VMEM((rows, width), BF16),
            pltpu.VMEM((rows, width), F32),
            pltpu.VMEM((bag * tiles, LANES), I32),
            pltpu.VMEM((bag, batch), BF16),
            pltpu.VMEM((1, batch), I32),
            pltpu.VMEM((padded, batch), I32),
            pltpu.VMEM((padded, batch), I32),
            pltpu.VMEM((2, BLOCK, LANES), I32),
            pltpu.VMEM((2, BLOCK, LANES), I32),
            pltpu.VMEM((PAIR * LANES, width), F32),
            pltpu.SMEM((2, BLOCK, LANES), I32),
            pltpu.SemaphoreType.DMA,
            pltpu.SemaphoreType.DMA((3,)),
            pltpu.SemaphoreType.DMA((2,)),
        ],
        compiler_params=pltpu.CompilerParams(vmem_limit_bytes=24 * 1024 * 1024),
        name="rank",
    )(*[pltpu.with_memory_space_constraint(x, pltpu.HBM) for x in operands])


def exchange_kernel(
    tables, t_hbm, keep_ref, ids_ref, lead_ref, over_ref, out_ref,
    t_bf, t_f32, gathered, pool, recv1, send2, recv2, ids_smem,
    t_sem, ids_sem, s1_send, s1_recv, s2_send, s2_recv,
):
    groups, part, width = recv1.shape
    ends, each = recv2.shape[:2]
    high = ends // tables
    batch = pool.shape[0]
    rows = t_f32.shape[0]
    chunks = t_sem.shape[0]
    chunk = rows // chunks
    table, row = lax.axis_index("table"), lax.axis_index("row")
    plane, place = row // groups, lax.rem(row, groups)

    def table_copy(c):
        span = pl.ds(c * chunk, chunk)
        return pltpu.make_async_copy(t_hbm.at[0, span], t_bf.at[span], t_sem.at[c])

    ids_copy = pltpu.make_async_copy(ids_ref, ids_smem, ids_sem)
    ids_copy.start()
    for c in range(chunks):
        table_copy(c).start()

    def plane_peer(d):
        return lax.rem(place + d, groups)

    def line_peer(d):
        return lax.rem(table + d // high, tables), lax.rem(plane + d % high, high)

    barrier = pltpu.get_barrier_semaphore()
    for d in range(1, groups):
        pl.semaphore_signal(
            barrier, inc=1, device_id=(table, plane * groups + plane_peer(d)), device_id_type=MESH
        )
    for d in range(1, ends):
        t, h = line_peer(d)
        pl.semaphore_signal(barrier, inc=1, device_id=(t, h * groups + place), device_id_type=MESH)

    bag_rows = lax.broadcasted_iota(I32, (batch, LANES), 0)
    lead = jnp.zeros((batch, LANES), F32)
    for tile in range(batch // LANES):
        lead = lead + jnp.where(
            bag_rows == bag_places(batch) + tile * 4, lead_ref[tile : tile + 1, :], 0.0
        )
    lead = lead.sum(axis=1, keepdims=True)

    for c in range(chunks):
        table_copy(c).wait()
        t_f32[c * chunk : (c + 1) * chunk, :] = t_bf[c * chunk : (c + 1) * chunk, :].astype(F32)
    ids_copy.wait()
    pool[...] = over_ref[...] + lead * t_f32[pl.ds(ids_smem[KEEP, 0], 1), :]
    for first in range(0, KEEP, PAIR):

        @pl.loop(0, PAIR * LANES, unroll=UNROLL)
        def _(u):
            source = ids_smem[first + u // LANES, u % LANES]
            gathered[pl.ds(first * LANES + u, 1), :] = t_f32[pl.ds(source, 1), :]

        pool[...] += jnp.dot(
            pick_bags([keep_ref[first + k : first + k + 1, :] for k in range(PAIR)], batch),
            gathered[first * LANES : (first + PAIR) * LANES, :].astype(BF16),
            preferred_element_type=F32,
        )

    pl.semaphore_wait(barrier, groups + ends - 2)

    def first_copy(d):
        peer = plane_peer(d)
        return pltpu.make_async_remote_copy(
            src_ref=pool.at[pl.ds(pl.multiple_of(peer * part, part), part)],
            dst_ref=recv1.at[d],
            send_sem=s1_send.at[d],
            recv_sem=s1_recv.at[d],
            device_id=(table, plane * groups + peer),
            device_id_type=MESH,
        )

    for d in range(1, groups):
        first_copy(d).start()
    total = pool[pl.ds(pl.multiple_of(place * part, part), part), :]
    for d in range(1, groups):
        first_copy(d).wait_recv()
        total = total + recv1[d]
    for q in range(ends):
        send2[q] = total[q * each : (q + 1) * each, :]

    def second_copy(d):
        t, h = line_peer(d)
        return pltpu.make_async_remote_copy(
            src_ref=send2.at[t * high + h],
            dst_ref=recv2.at[d],
            send_sem=s2_send.at[d],
            recv_sem=s2_recv.at[d],
            device_id=(t, h * groups + place),
            device_id_type=MESH,
        )

    for d in range(1, ends):
        second_copy(d).start()
    recv2[0] = send2[table * high + plane]
    for d in range(1, ends):
        second_copy(d).wait_recv()
    for dt in range(tables):
        source = lax.rem(table - dt + tables, tables)
        value = recv2[dt * high]
        for dh in range(1, high):
            value = value + recv2[dt * high + dh]
        out_ref[source] = value.astype(BF16)
    for d in range(1, groups):
        first_copy(d).wait_send()
    for d in range(1, ends):
        second_copy(d).wait_send()


def exchange(table_rows, keep, ids, lead, over, tables, groups, ends):
    rows, width = table_rows.shape[1:]
    batch = over.shape[0]
    part = batch // groups
    each = part // ends
    vmem = pl.BlockSpec(memory_space=pltpu.VMEM)
    return pl.pallas_call(
        functools.partial(exchange_kernel, tables),
        out_shape=jax.ShapeDtypeStruct((tables, each, width), BF16),
        in_specs=[pl.BlockSpec(memory_space=pltpu.HBM)] + [vmem] * 4,
        out_specs=vmem,
        scratch_shapes=[
            pltpu.VMEM((rows, width), BF16),
            pltpu.VMEM((rows, width), F32),
            pltpu.VMEM((KEEP * LANES, width), F32),
            pltpu.VMEM((batch, width), F32),
            pltpu.VMEM((groups, part, width), F32),
            pltpu.VMEM((ends, each, width), F32),
            pltpu.VMEM((ends, each, width), F32),
            pltpu.SMEM((KEEP + 8, LANES), I32),
            pltpu.SemaphoreType.DMA((4,)),
            pltpu.SemaphoreType.DMA,
            pltpu.SemaphoreType.DMA((groups,)),
            pltpu.SemaphoreType.DMA((groups,)),
            pltpu.SemaphoreType.DMA((ends,)),
            pltpu.SemaphoreType.DMA((ends,)),
        ],
        compiler_params=pltpu.CompilerParams(
            collective_id=0, has_side_effects=True, vmem_limit_bytes=24 * 1024 * 1024
        ),
        name="exchange",
    )(pltpu.with_memory_space_constraint(table_rows, pltpu.HBM), keep, ids, lead, over)


def on_device(tables, indices, weights, lengths):
    picked = rank(tables, indices, weights, lengths)
    return exchange(tables, *picked, lax.axis_size("table"), 32, 8)


def solution(mesh):
    placed = (
        P("table", "row", None),
        P("table", None, None),
        P("table", None, None),
        P("table", None),
    )
    return jax.shard_map(
        on_device,
        mesh=mesh,
        in_specs=placed,
        out_specs=P(None, ("table", "row"), None),
        check_vma=False,
    )
```

time: 25.9 us -> 24.3 us (0.938)
  Pallas kernels: 25.3 us -> 23.5 us
    pallas_call x1, Pallas kernels: 3.22 us -> 1.97 us  [rank(): pl.pallas_call(rank_kernel, out_shape=(jax.ShapeDtypeStruct((KEEP, LANES)...]
    pallas_call x1, Pallas kernels: 22.1 us -> 21.6 us  [exchange(): pl.pallas_call(functools.partial(exchange_kernel, tables), out_shape=jax....]
where the time goes in v1:
time: 24.3 us; the launch traced here: 24.1 us
  Pallas kernels  23.5 us (97%)
  local copies, waits for them, and re-layouts  0.58 us (2%)
    pallas_call x1, Pallas kernels, exchange(): pl.pallas_call(functools.partial(exchange_kernel, tables), out_shape=jax....  21.6 us
    pallas_call x1, Pallas kernels, rank(): pl.pallas_call(rank_kernel, out_shape=(jax.ShapeDtypeStruct((KEEP, LANES)...  1.97 us
    unnamed x1, local copies, waits for them, and re-layouts  0.58 us

profile of v1, /device:TPU:1, one launch (start us, length us, event | category | flops | bytes accessed | tf_op | source)
XLA Modules:
  0.0 24.1 jit_solution(5993438570308064827)
XLA Ops:
  0.0 2.0 %rank.1 = (s32[16,128]{1,0:T(8,128)S(1)}, s32[24,128]{1,0:T(8,128)S(1)}, f32[8,128]{1,0:T(8,128)S(1)}, f32[512,128]{1,0:T(8,128)S(1)}) custom-call(bf16[1,8192,128]{2,1,0:T(8,128)(2,1)} %t_hbm.3, s32[400,128]{1,0:T(8,128)} %bitcast.1, bf16[1,100,512]{2,1,0:T(8,128)(2,1)} %w_hbm.1, s32[1,512]{1,0:T(1,128)} %l_hbm.1), custom_call_target="tpu_custom_call" | custom-call | tf_op jit(solution)/shard_map/rank/pallas_call | solution.py:175
  2.0 21.6 %exchange.1 = bf16[4,2,128]{2,1,0:T(2,128)(2,1)S(1)} custom-call(bf16[1,8192,128]{2,1,0:T(8,128)(2,1)} %t_hbm.3, s32[16,128]{1,0:T(8,128)S(1)} %get-tuple-element.9.keep_ref, s32[24,128]{1,0:T(8,128)S(1)} %get-tuple-element.10.ids_ref, f32[8,128]{1,0:T(8,128)S(1)} %get-tuple-element.11.lead_ref, f32[512,128]{1,0:T(8,128)S(1)} %get-tuple-element.12.over_ref), custom_call_target="tpu_custom_call" | custom-call | tf_op jit(solution)/shard_map/exchange/pallas_call | solution.py:327
  23.6 0.6 %copy.6 = bf16[4,2,128]{2,1,0:T(2,128)(2,1)} copy(bf16[4,2,128]{2,1,0:T(2,128)(2,1)S(1)} %exchange.1) | data formatting | bytes 4096
